TPU v7x, 32 devices: a whole 2x2x4 slice. The times are simulated.
32 devices in a mesh: grid: 8 (over z, x), orb: 4 (over y, core).
Axes of the slice: x: 2, y: 2, z: 4, core: 2. Of those that a mesh axis runs over, the one named last changes fastest.
Arguments:
- orbitals: bfloat16 [1800, 65536], P('orb', 'grid'), may hold values from -0.5 to 1.5
- pivots: int32 [3, 96], replicated, may hold values from 0 to 65535, as said below
Outputs:
- cholesky_factor: float32 [65536, 288], P(('grid', 'orb'))
- residual_diagonal: float32 [65536], P(('grid', 'orb'))
- diagonal_peaks: float32 [3], replicated
Inputs may be any that keep to these rules, and one draw needn't show every extreme that they name: `pivots`: all 3 x 96 pivot indices are distinct grid points.
All inputs are finite; a program needn't handle non-finite values.
Results may differ from a plain program's by a relative error of at most 0.0003.
Values may be sent and summed in bfloat16 or wider, within the bound.
A program may use at most 64 MiB of HBM per device.

v0:
```python
import jax
import jax.numpy as jnp
from jax import lax
from jax.sharding import PartitionSpec as P

ORB = 1800


def pick_columns(values, index, base, count):
    local = index - base
    inside = (local >= 0) & (local < count)
    taken = jnp.take(values, jnp.clip(local, 0, count - 1), axis=1)
    return jnp.where(inside[None, :], taken, jnp.zeros_like(taken))


def contract_first(left, right):
    return lax.dot_general(
        left, right, (((0,), (0,)), ((), ())), preferred_element_type=jnp.float32
    )


def on_device(orbitals, pivots):
    rows = orbitals.shape[1]
    groups = lax.axis_size("orb")
    share = rows // groups
    sections = pivots.shape[0]
    count = pivots.shape[1]
    total_rank = sections * count
    grid_base = lax.axis_index("grid") * rows
    squares = lax.psum_scatter(
        jnp.sum(jnp.square(orbitals.astype(jnp.float32)), axis=0),
        "orb",
        scatter_dimension=0,
        tiled=True,
    )
    diagonal = jnp.square(squares / ORB)
    factor = jnp.zeros((share, total_rank), jnp.float32)
    flat = pivots.reshape(total_rank)
    local_pivots = lax.psum(
        pick_columns(orbitals, flat, grid_base, rows).astype(jnp.float32).astype(jnp.bfloat16),
        "grid",
    )
    whole = lax.all_gather(local_pivots, "orb", axis=0, tiled=True)
    pivot_pairs = contract_first(whole, whole)
    pivot_factor = jnp.zeros((total_rank, total_rank), jnp.float32)
    peaks = []
    for section in range(sections):
        lead = section * count
        sampled_here = lax.slice_in_dim(local_pivots, lead, lead + count, axis=1)
        known = lax.slice_in_dim(pivot_factor, lead, lead + count, axis=0)
        pair = lax.slice_in_dim(
            lax.slice_in_dim(pivot_pairs, lead, lead + count, axis=0), lead, lead + count, axis=1
        )

        def product(start, length, picked=sampled_here):
            return contract_first(orbitals, picked)

        inner = lax.psum_scatter(
            product(jnp.int32(0), share * lax.axis_size("orb")),
            "orb",
            scatter_dimension=0,
            tiled=True,
        )
        block = jnp.square(pair / ORB) - jnp.dot(known, known.T, precision=lax.Precision.HIGHEST)
        columns = jnp.square(inner / ORB) - jnp.dot(
            factor, known.T, precision=lax.Precision.HIGHEST
        )
        lower = jnp.linalg.cholesky(block)
        fresh = jax.scipy.linalg.solve_triangular(lower, columns.T, lower=True).T
        factor = factor.at[:, lead : lead + count].set(fresh)
        pivot_columns = jnp.square(
            lax.slice_in_dim(pivot_pairs, lead, lead + count, axis=1) / ORB
        ) - jnp.dot(pivot_factor, known.T, precision=lax.Precision.HIGHEST)
        pivot_fresh = jax.scipy.linalg.solve_triangular(lower, pivot_columns.T, lower=True).T
        pivot_factor = pivot_factor.at[:, lead : lead + count].set(pivot_fresh)
        diagonal = diagonal - jnp.sum(fresh * fresh, axis=1)
        peaks.append(lax.pmax(jnp.max(diagonal), ("grid", "orb")))
    peak_values = jnp.stack(peaks)
    return (factor, diagonal, peak_values)


def solution(mesh):
    in_specs = (P("orb", "grid"), P())
    out_specs = (P(("grid", "orb"), None), P(("grid", "orb")), P())
    return jax.shard_map(
        on_device, mesh=mesh, in_specs=in_specs, out_specs=out_specs, check_vma=False
    )
```

profile of v0, /device:TPU:0, one launch (start us, length us, event | category | flops | bytes accessed | tf_op | source)
XLA Modules:
  0.0 281.3 jit_solution(3974365267938279486)
XLA Ops:
  8.8 11.6 %copy.26 = bf16[450,8192]{0,1:T(8,128)(2,1)} copy(bf16[450,8192]{1,0:T(8,128)(2,1)} %param.17) | data formatting | bytes 14745600 | tf_op args[0]
  20.5 6.5 %gather_fusion = bf16[288,450]{1,0:T(8,128)(2,1)S(1)} fusion(bf16[450,8192]{0,1:T(8,128)(2,1)} %copy.26, s32[1024]{0:T(1024)S(1)} %pad_clamp_fusion), kind=kCustom, calls=%fused_computation | custom fusion | bytes 519552 | tf_op jit(solution)/shard_map/jit(_take)/gather | solution.py:12
  27.9 74.2 %all-reduce.6.cloned.1.call-done = bf16[450,288]{0,1:T(8,128)(2,1)} async-done(((bf16[450,288]{0,1:T(8,128)(2,1)}), bf16[450,288]{0,1:T(8,128)(2,1)}) %all-reduce.6.cloned.1.call-update) | async-done | bytes 259216 | tf_op jit(solution)/shard_map/psum | solution.py:39
  102.1 6.3 %convolution_bitcast_fusion.2 = f32[8192,96]{0,1:T(8,128)} fusion(bf16[450,8192]{1,0:T(8,128)(2,1)} %param.17, bf16[450,288]{0,1:T(8,128)(2,1)} %all-reduce.6.cloned.1.call-done), kind=kOutput, calls=%fused_computation.4 | convolution fusion | flops 707788800 | bytes 10715136 | tf_op jit(solution)/shard_map/dot_general | solution.py:17
  109.4 6.4 %convolution_bitcast_fusion.1 = f32[8192,96]{0,1:T(8,128)} fusion(bf16[450,8192]{1,0:T(8,128)(2,1)} %param.17, bf16[450,288]{0,1:T(8,128)(2,1)S(1)} %copy-done.2), kind=kOutput, calls=%fused_computation.3 | convolution fusion | flops 707788800 | bytes 10616832 | tf_op jit(solution)/shard_map/dot_general | solution.py:17
  115.8 6.6 %convolution_bitcast_fusion = f32[8192,96]{0,1:T(8,128)} fusion(bf16[450,8192]{1,0:T(8,128)(2,1)} %param.17, bf16[450,288]{0,1:T(8,128)(2,1)S(1)} %copy-done.2), kind=kOutput, calls=%fused_computation.2 | convolution fusion | flops 707788800 | bytes 10616832 | tf_op jit(solution)/shard_map/dot_general | solution.py:17
  125.7 4.8 %multiply_reduce_fusion = f32[8192]{0:T(1024)S(1)} fusion(bf16[450,8192]{1,0:T(8,128)(2,1)} %param.17), kind=kLoop, calls=%fused_computation.1 | loop fusion | flops 11051008 | bytes 7405568 | tf_op jit(solution)/shard_map/reduce_sum | solution.py:31
  130.5 12.2 %all-reduce.2 = f32[8192]{0:T(1024)S(1)} all-reduce(f32[8192]{0:T(1024)S(1)} %multiply_reduce_fusion), channel_id=5, replica_groups=mesh['grid'=8,'orb'=4] {'orb'}, use_global_device_ids=true, to_apply=%region_9.13.clone | all-reduce | flops 8192 | bytes 65536
  142.7 10.8 %all-gather = bf16[4,450,288]{1,2,0:T(8,128)(2,1)S(1)} all-gather(bf16[1,450,288]{1,2,0:T(8,128)(2,1)S(1)} %bitcast.91), channel_id=1, replica_groups=mesh['grid'=8,'orb'=4] {'orb'}, dimensions={0}, use_global_device_ids=true | all-gather | bytes 1296000 | tf_op jit(solution)/shard_map/all_gather | solution.py:43
  154.3 1.6 reshape.196
  157.3 8.8 %cholesky.59 = f32[96,96]{1,0:T(8,128)S(1)} custom-call(f32[96,96]{1,0:T(8,128)S(1)} %fusion.36), custom_call_target="Cholesky" | custom-call | tf_op jit(solution)/shard_map/jit(cholesky)/cholesky | solution.py:68
  167.4 7.4 %custom-call.11 = f32[1,96,96]{1,2,0:T(8,128)S(1)} custom-call(f32[1,96,96]{2,1,0:T(8,128)S(1)} %fusion.25), custom_call_target="InvertDiagBlocksLowerTriangular" | custom-call | tf_op jit(solution)/shard_map/jit(_solve_triangular)/triangular_solve | solution.py:69
  176.4 8.8 %cholesky.70 = f32[96,96]{1,0:T(8,128)S(1)} custom-call(f32[96,96]{1,0:T(8,128)S(1)} %fusion.33), custom_call_target="Cholesky" | custom-call | tf_op jit(solution)/shard_map/jit(cholesky)/cholesky | solution.py:68
  186.5 7.4 %custom-call.13 = f32[1,96,96]{1,2,0:T(8,128)S(1)} custom-call(f32[1,96,96]{2,1,0:T(8,128)S(1)} %fusion.26), custom_call_target="InvertDiagBlocksLowerTriangular" | custom-call | tf_op jit(solution)/shard_map/jit(_solve_triangular)/triangular_solve | solution.py:69
  196.3 8.9 %cholesky.81 = f32[96,96]{1,0:T(8,128)S(1)} custom-call(f32[96,96]{1,0:T(8,128)S(1)} %fusion.29), custom_call_target="Cholesky" | custom-call | tf_op jit(solution)/shard_map/jit(cholesky)/cholesky | solution.py:68
  206.5 7.4 %custom-call.15 = f32[1,96,96]{1,2,0:T(8,128)S(1)} custom-call(f32[1,96,96]{2,1,0:T(8,128)S(1)} %fusion.27), custom_call_target="InvertDiagBlocksLowerTriangular" | custom-call | tf_op jit(solution)/shard_map/jit(_solve_triangular)/triangular_solve | solution.py:69
  213.9 2.6 multiply_reduce_fusion.3
  216.9 2.3 fusion.1
  219.2 1.5 bitcast_dynamic-update-slice_fusion
  220.8 5.8 %reduce-scatter.8.cloned.1.call-done = f32[2048,96]{0,1:T(8,128)} async-done(((f32[8192,96]{0,1:T(8,128)}), f32[2048,96]{0,1:T(8,128)}) %reduce-scatter.8.cloned.1.call-update) | async-done | bytes 786448 | tf_op jit(solution)/shard_map/reduce_scatter | solution.py:58
  226.5 3.3 %fusion = f32[96,2048]{1,0:T(8,128)S(1)} fusion(f32[2048,288]{0,1:T(8,128)S(1)} %get-tuple-element.81, f32[2048,96]{0,1:T(8,128)} %reduce-scatter.8.cloned.1.call-done, f32[288,288]{0,1:T(8,128)} %copy-done.1), kind=kOutput, calls=%fused_computation.7 | convolution fusion | flops 680067072 | bytes 4079616 | tf_op jit(solution)/shard_map/dot_general | solution.py:65
  231.5 1.2 fusion.48
  232.7 39.6 %all-reduce.3 = (f32[1]{0:T(128)}, f32[1]{0:T(128)}, f32[1]{0:T(128)}) all-reduce(f32[1]{0:T(128)} %bitcast.30, f32[1]{0:T(128)} %bitcast.29, f32[1]{0:T(128)} %bitcast.28), channel_id=1, replica_groups=mesh['grid'=8,'orb'=4] {'grid','orb'}, use_global_device_ids=true, to_apply=%region_18.22 | all-reduce | flops 3 | bytes 24 | tf_op jit(solution)/shard_map/pmax | solution.py:77
  272.3 2.5 pad_maximum_fusion
  (62 shorter events, 18.3 us)
Async XLA Ops:
  7.2 94.9 %all-reduce.6.cloned.1.call-start = ((), (), s32[]{:S(2)}) async-start(), calls=%async_computation.3 | async-start | bytes 589824 | tf_op jit(solution)/shard_map/psum | solution.py:39
  27.9 186.0 %reduce-scatter.4.cloned.1.call-start = ((), (), s32[]{:S(2)}) async-start(), calls=%async_computation.4 | async-start | bytes 3932160 | tf_op jit(solution)/shard_map/reduce_scatter | solution.py:58
  108.4 1.0 copy-start.2
  108.4 108.4 %reduce-scatter.6.cloned.1.call-start = ((), (), s32[]{:S(2)}) async-start(), calls=%async_computation.5 | async-start | bytes 3932160 | tf_op jit(solution)/shard_map/reduce_scatter | solution.py:58
  115.8 110.8 %reduce-scatter.8.cloned.1.call-start = ((), (), s32[]{:S(2)}) async-start(), calls=%async_computation.6 | async-start | bytes 3932160 | tf_op jit(solution)/shard_map/reduce_scatter | solution.py:58
  122.5 0.7 copy-start.3
  195.6 21.0 %copy-start.1 = (f32[288,288]{0,1:T(8,128)}, f32[288,288]{0,1:T(8,128)S(1)}, u32[]{:S(2)}) copy-start(f32[288,288]{0,1:T(8,128)S(1)} %fusion.4) | copy-start | bytes 995332
  230.7 44.1 %copy-start = (f32[2048,288]{0,1:T(8,128)}, f32[2048,288]{0,1:T(8,128)S(1)}, u32[]{:S(2)}) copy-start(f32[2048,288]{0,1:T(8,128)S(1)} %get-tuple-element.77) | copy-start | bytes 7077892
Sparse Core Ops, SparseCore 0:
  28.0 74.0 all-reduce.5
  108.6 37.2 reduce-scatter.3
  148.4 37.8 reduce-scatter.5
  188.7 37.7 reduce-scatter.7
where the time goes:
time: 282 us; the launch traced here: 281 us
  waiting for transfers between devices  80.1 us (28%)
  other arithmetic  65.5 us (23%)
  blocking collectives  62.5 us (22%)
  matrix products  34.5 us (12%)
  local copies, waits for them, and re-layouts  23.8 us (8%)
  between operations  14.8 us (5%)
    psum x1, waiting for transfers between devices, on_device(): lax.psum(pick_columns(orbitals, flat, grid_base, rows).astype(jnp.float32...  74.2 us
    pmax x1, blocking collectives, on_device(): peaks.append(lax.pmax(jnp.max(diagonal), ('grid', 'orb')))  39.6 us
    another operation x9, other arithmetic, on_device(): lower = jnp.linalg.cholesky(block)  28.5 us
    another operation x6, other arithmetic, on_device(): fresh = jax.scipy.linalg.solve_triangular(lower, columns.T, lower=True).T  24 us
    dot_general x4, matrix products, contract_first(): lax.dot_general(left, right, (((0,), (0,)), ((), ())), preferred_element_...  20.1 us
    unnamed x14, local copies, waits for them, and re-layouts  15.5 us
    unnamed x1, blocking collectives  12.2 us
    all_gather x1, blocking collectives, on_device(): whole = lax.all_gather(local_pivots, 'orb', axis=0, tiled=True)  10.8 us
  transfers between devices with their start and end apart: 4, of which 2 were waited for; matrix products, arithmetic and copies ran while one was open for 31% of the time, Pallas kernels for 0%

commit v1 on v0

v1 whole, which is shorter than its diff:
```python
import functools

import jax
import jax.numpy as jnp
from jax import lax
from jax.experimental import pallas as pl
from jax.experimental.pallas import tpu as pltpu
from jax.sharding import PartitionSpec as P

F32 = jnp.float32
BF16 = jnp.bfloat16
HIGHEST = lax.Precision.HIGHEST
MESH = pl.DeviceIdType.MESH
BLOCK = 48
PARTS = 4


def dot_nn(a, b, precision=None):
    return lax.dot_general(
        a, b, (((1,), (0,)), ((), ())), precision=precision, preferred_element_type=F32
    )


def dot_nt(a, b, precision=None):
    return lax.dot_general(
        a, b, (((1,), (1,)), ((), ())), precision=precision, preferred_element_type=F32
    )


def dot_tn(a, b, precision=None):
    return lax.dot_general(
        a, b, (((0,), (0,)), ((), ())), precision=precision, preferred_element_type=F32
    )


def eliminate_small(t, size):
    row_at = lax.broadcasted_iota(jnp.int32, t.shape, 0)
    for k in range(size):
        scale = lax.rsqrt(t[k : k + 1, k : k + 1])
        row = t[k : k + 1, :] * scale
        column = t[:, k : k + 1] * scale
        t = jnp.where(row_at > k, t - column * row, jnp.where(row_at == k, row, t))
    return t


def kernel(
    n_grid, n_orb, steps, orbitals_count,
    orb_hbm, piv_ref,
    factor_hbm, diag_ref, peaks_ref,
    own, other, mine, total, heard, swap, sums, arrived, local, pair_send, pair_recv,
    aug, out_v, tile_mine, tile_orb, tile_grid,
    load_sem, out_sem, x_send, x_recv, p1_send, p1_recv, p2_send, p2_recv,
    c_send, c_recv, q_send, q_recv, h_send, h_recv, s_send, s_recv,
    mo_send, mo_recv, mg_send, mg_recv,
):
    g = lax.axis_index("grid")
    o = lax.axis_index("orb")
    core = lax.rem(o, 2)
    side = o // 2
    mate = o + 1 - 2 * core
    across = (1 - side) * 2 + core
    share = own.shape[2]
    slots, slot_rows, _ = mine.shape
    rank = slots * slot_rows
    part = share // PARTS
    rows = share * n_orb

    loads = []
    for b in range(n_orb):
        copy = pltpu.make_async_copy(
            orb_hbm.at[:, pl.ds(b * share, share)], own.at[b], load_sem.at[b]
        )
        copy.start()
        loads.append(copy)

    barrier = pltpu.get_barrier_semaphore()
    for d in range(1, n_grid):
        pl.semaphore_signal(
            barrier, inc=1, device_id=(lax.rem(g + d, n_grid), o), device_id_type=MESH
        )
    for d in range(1, n_orb):
        pl.semaphore_signal(
            barrier, inc=1, device_id=(g, lax.rem(o + d, n_orb)), device_id_type=MESH
        )
    pl.semaphore_wait(barrier, n_grid + n_orb - 2)

    crossing = []
    for yy in range(2):
        start = pl.multiple_of((yy * 2 + 1 - core) * share, share)
        copy = pltpu.make_async_remote_copy(
            src_ref=orb_hbm.at[:, pl.ds(start, share)],
            dst_ref=other.at[yy],
            send_sem=x_send.at[yy],
            recv_sem=x_recv.at[yy],
            device_id=(g, mate),
            device_id_type=MESH,
        )
        copy.start()
        crossing.append(copy)

    base = g * rows
    wanted = piv_ref[...] - base
    picked = None
    for b in range(n_orb):
        loads[b].wait()
        lanes = lax.broadcasted_iota(jnp.int32, (rank, share), 1) + b * share
        hot = jnp.where(lanes == wanted, 1.0, 0.0).astype(BF16)
        term = dot_nt(hot, own[b])
        picked = term if picked is None else picked + term
    picked = picked.astype(BF16)
    for s in range(slots):
        mine[s] = picked[s * slot_rows : (s + 1) * slot_rows]

    def first(d):
        target = lax.rem(g + d, n_grid)
        return target, pltpu.make_async_remote_copy(
            src_ref=mine.at[lax.rem(target, slots)],
            dst_ref=heard.at[d],
            send_sem=p1_send.at[d],
            recv_sem=p1_recv.at[d],
            device_id=(target, o),
            device_id_type=MESH,
        )

    def second(d):
        target = lax.rem(g + d, n_grid)
        return pltpu.make_async_remote_copy(
            src_ref=heard.at[0],
            dst_ref=total.at[lax.rem(g, slots)],
            send_sem=p2_send.at[d],
            recv_sem=p2_recv.at[d],
            device_id=(target, o),
            device_id_type=MESH,
        )

    for d in range(1, n_grid):
        target, copy = first(d)

        @pl.when(target < slots)
        def _(copy=copy):
            copy.start()

    @pl.when(g < slots)
    def _():
        added = mine[lax.rem(g, slots)]
        for d in range(1, n_grid):
            first(d)[1].wait_recv()
            added = added + heard[d]
        heard[0] = added
        for d in range(1, n_grid):
            second(d).start()
        total[lax.rem(g, slots)] = added

    for d in range(1, n_grid):
        source = lax.rem(g + n_grid - d, n_grid)

        @pl.when(source < slots)
        def _(d=d):
            second(d).wait_recv()

    swap_copy = pltpu.make_async_remote_copy(
        src_ref=total, dst_ref=swap, send_sem=c_send, recv_sem=c_recv,
        device_id=(g, mate), device_id_type=MESH,
    )
    swap_copy.start()
    here = jnp.reshape(total[...], (rank, total.shape[2]))
    pair_here = dot_nt(here, here)
    swap_copy.wait_recv()
    there = jnp.reshape(swap[...], (rank, swap.shape[2]))
    pair = pair_here + dot_nt(there, there)
    half = rank // 2
    for h in range(2):
        pair_send[h] = pair[h * half : (h + 1) * half]
    pair_copy = pltpu.make_async_remote_copy(
        src_ref=pair_send.at[core], dst_ref=pair_recv.at[0], send_sem=q_send, recv_sem=q_recv,
        device_id=(g, across), device_id_type=MESH,
    )
    pair_copy.start()

    for copy in crossing:
        copy.wait_recv()

    def products(block, yy, p):
        lo = p * part
        a = own[block, :, lo : lo + part]
        b = other[yy, :, lo : lo + part]
        inner = dot_nn(here, a) + dot_nn(there, b)
        a32 = a.astype(F32)
        b32 = b.astype(F32)
        squares = jnp.sum(a32 * a32, axis=0, keepdims=True) + jnp.sum(
            b32 * b32, axis=0, keepdims=True
        )
        return inner, squares

    travel = []
    for p in range(PARTS):
        inner, squares = products(across, 1 - side, p)
        sums[p, 0:rank, :] = inner
        sums[p, rank : rank + 8, :] = jnp.broadcast_to(squares, (8, part))
        copy = pltpu.make_async_remote_copy(
            src_ref=sums.at[p], dst_ref=arrived.at[p],
            send_sem=s_send.at[p], recv_sem=s_recv.at[p],
            device_id=(g, across), device_id_type=MESH,
        )
        copy.start()
        travel.append(copy)

    pair_copy.wait_recv()
    half_copy = pltpu.make_async_remote_copy(
        src_ref=pair_recv.at[0], dst_ref=pair_recv.at[1], send_sem=h_send, recv_sem=h_recv,
        device_id=(g, mate), device_id_type=MESH,
    )
    half_copy.start()
    for p in range(PARTS):
        inner, squares = products(o, side, p)
        local[p, 0:rank, :] = inner
        local[p, rank : rank + 8, :] = jnp.broadcast_to(squares, (8, part))
    half_copy.wait_recv()
    first_half = jnp.where(core == 0, pair_recv[0], pair_recv[1])
    second_half = jnp.where(core == 0, pair_recv[1], pair_recv[0])
    wide = aug.shape[1] // 2
    aug[:, wide:] = jnp.where(
        lax.broadcasted_iota(jnp.int32, (rank, wide), 0)
        == lax.broadcasted_iota(jnp.int32, (rank, wide), 1),
        1.0,
        0.0,
    )
    aug[:, :wide] = jnp.zeros((rank, wide), F32)
    aug[0:half, 0:rank] = jnp.square((pair_send[0] + first_half) / orbitals_count)
    aug[half:rank, 0:rank] = jnp.square((pair_send[1] + second_half) / orbitals_count)

    def block_step(j, carry):
        start = pl.multiple_of(j * BLOCK, BLOCK)
        strip = aug[pl.ds(start, BLOCK), :]
        pick = jnp.where(
            lax.broadcasted_iota(jnp.int32, (wide, 128), 0)
            == lax.broadcasted_iota(jnp.int32, (wide, 128), 1) + start,
            1.0,
            0.0,
        )
        lane = lax.broadcasted_iota(jnp.int32, (BLOCK, 128), 1)
        row_at = lax.broadcasted_iota(jnp.int32, (BLOCK, 128), 0)
        square = dot_nn(strip[:, :wide], pick, HIGHEST)
        tile = jnp.where(lane < BLOCK, square, jnp.where(lane == row_at + 64, 1.0, 0.0))
        tile = eliminate_small(tile, BLOCK)
        inverse = tile[:, 64 : 64 + BLOCK]
        solved = dot_nn(inverse, strip, HIGHEST)
        head = solved[:, :wide]
        ahead = lax.broadcasted_iota(jnp.int32, (BLOCK, wide), 1) >= start + BLOCK
        multipliers = jnp.where(ahead, head, 0.0)
        aug[...] = aug[...] - dot_tn(multipliers, solved, HIGHEST)[0:rank]
        aug[pl.ds(start, BLOCK), :] = solved
        return carry

    lax.fori_loop(0, rank // BLOCK, block_step, 0)
    lower_inverse = aug[:, wide:]

    count = rank // steps
    best = [None] * steps
    stores = []
    for p in range(PARTS):
        travel[p].wait_recv()
        both = local[p] + arrived[p]
        scaled = jnp.square(both / orbitals_count)
        columns = scaled[0:rank]
        diagonal = scaled[rank : rank + 1]
        solved = dot_nn(lower_inverse[:, 0:rank], columns, HIGHEST)
        out_v[p] = solved.T
        store = pltpu.make_async_copy(
            out_v.at[p], factor_hbm.at[pl.ds(p * part, part), :], out_sem.at[p]
        )
        store.start()
        stores.append(store)
        for s in range(steps):
            piece = solved[s * count : (s + 1) * count]
            diagonal = diagonal - jnp.sum(piece * piece, axis=0, keepdims=True)
            best[s] = diagonal if best[s] is None else jnp.maximum(best[s], diagonal)
        diag_ref[:, p * part : (p + 1) * part] = diagonal

    row8 = lax.broadcasted_iota(jnp.int32, (8, 128), 0)
    tile = jnp.zeros((8, 128), F32)
    for s in range(steps):
        top = jnp.max(best[s], axis=1, keepdims=True)
        tile = jnp.where(row8 == s, jnp.broadcast_to(top, (8, 128)), tile)
    tile_mine[0] = tile
    round_orb = []
    for d in range(1, n_orb):
        copy = pltpu.make_async_remote_copy(
            src_ref=tile_mine.at[0], dst_ref=tile_orb.at[d],
            send_sem=mo_send.at[d], recv_sem=mo_recv.at[d],
            device_id=(g, lax.rem(o + d, n_orb)), device_id_type=MESH,
        )
        copy.start()
        round_orb.append(copy)
    for d in range(1, n_orb):
        round_orb[d - 1].wait_recv()
        tile = jnp.maximum(tile, tile_orb[d])
    tile_mine[1] = tile
    round_grid = []
    for d in range(1, n_grid):
        copy = pltpu.make_async_remote_copy(
            src_ref=tile_mine.at[1], dst_ref=tile_grid.at[d],
            send_sem=mg_send.at[d], recv_sem=mg_recv.at[d],
            device_id=(lax.rem(g + d, n_grid), o), device_id_type=MESH,
        )
        copy.start()
        round_grid.append(copy)
    for d in range(1, n_grid):
        round_grid[d - 1].wait_recv()
        tile = jnp.maximum(tile, tile_grid[d])
    peaks_ref[...] = tile

    for store in stores:
        store.wait()
    for d in range(1, n_grid):
        target, copy = first(d)

        @pl.when(target < slots)
        def _(copy=copy):
            copy.wait_send()

    @pl.when(g < slots)
    def _():
        for d in range(1, n_grid):
            second(d).wait_send()

    for copy in crossing + [swap_copy, pair_copy, half_copy] + travel + round_orb + round_grid:
        copy.wait_send()


def solution(mesh):
    n_grid, n_orb = mesh.shape["grid"], mesh.shape["orb"]
    assert n_orb == 4

    def on_device(orbitals, pivots):
        depth, rows = orbitals.shape
        steps, count = pivots.shape
        rank = steps * count
        share = rows // n_orb
        part = share // PARTS
        slot_rows = -(-rank // n_grid)
        slot_rows = -(-slot_rows // 16) * 16
        while rank % slot_rows:
            slot_rows += 16
        slots = rank // slot_rows
        wide = -(-rank // 128) * 128
        dma = pltpu.SemaphoreType.DMA
        vmem = pltpu.VMEM
        factor, diagonal, peaks = pl.pallas_call(
            functools.partial(kernel, n_grid, n_orb, steps, depth * n_orb),
            out_shape=(
                jax.ShapeDtypeStruct((share, rank), F32),
                jax.ShapeDtypeStruct((1, share), F32),
                jax.ShapeDtypeStruct((8, 128), F32),
            ),
            in_specs=[
                pl.BlockSpec(memory_space=pl.ANY),
                pl.BlockSpec(memory_space=vmem),
            ],
            out_specs=(
                pl.BlockSpec(memory_space=pl.ANY),
                pl.BlockSpec(memory_space=vmem),
                pl.BlockSpec(memory_space=vmem),
            ),
            scratch_shapes=[
                vmem((n_orb, depth, share), BF16),
                vmem((2, depth, share), BF16),
                vmem((slots, slot_rows, depth), BF16),
                vmem((slots, slot_rows, depth), BF16),
                vmem((n_grid, slot_rows, depth), BF16),
                vmem((slots, slot_rows, depth), BF16),
                vmem((PARTS, rank + 8, part), F32),
                vmem((PARTS, rank + 8, part), F32),
                vmem((PARTS, rank + 8, part), F32),
                vmem((2, rank // 2, rank), F32),
                vmem((2, rank // 2, rank), F32),
                vmem((rank, 2 * wide), F32),
                vmem((PARTS, part, rank), F32),
                vmem((2, 8, 128), F32),
                vmem((n_orb, 8, 128), F32),
                vmem((n_grid, 8, 128), F32),
                dma((n_orb,)), dma((PARTS,)), dma((2,)), dma((2,)),
                dma((n_grid,)), dma((n_grid,)), dma((n_grid,)), dma((n_grid,)),
                dma, dma, dma, dma, dma, dma, dma((PARTS,)), dma((PARTS,)),
                dma((n_orb,)), dma((n_orb,)), dma((n_grid,)), dma((n_grid,)),
            ],
            compiler_params=pltpu.CompilerParams(
                collective_id=0, has_side_effects=True, vmem_limit_bytes=58 * 1024 * 1024
            ),
        )(orbitals, pivots.reshape(rank, 1))
        return factor, diagonal.reshape(share), peaks[:steps, 0]

    return jax.shard_map(
        on_device,
        mesh=mesh,
        in_specs=(P("orb", "grid"), P()),
        out_specs=(P(("grid", "orb"), None), P(("grid", "orb")), P()),
        check_vma=False,
    )
```

time: 282 us -> 105 us (0.37)
  Pallas kernels: 0 us -> 98.1 us
  waiting for transfers between devices: 80.1 us -> 0 us
  other arithmetic: 65.5 us -> 0 us
  blocking collectives: 62.5 us -> 0 us
  matrix products: 34.5 us -> 0 us
  local copies, waits for them, and re-layouts: 23.8 us -> 6.1 us
  between operations: 14.8 us -> 0.66 us
    pallas_call x0 -> x1, Pallas kernels: none -> 98.1 us  [on_device(): pl.pallas_call(functools.partial(kernel, n_grid, n_orb, steps, depth * n_...]
    psum x1 -> x0, waiting for transfers between devices: 74.2 us -> none  [on_device(): lax.psum(pick_columns(orbitals, flat, grid_base, rows).astype(jnp.float32...]
    another operation x18 -> x0, other arithmetic: 56.3 us -> none  [the longest x9 28.5 us: on_device(): lower = jnp.linalg.cholesky(block)]
    pmax x1 -> x0, blocking collectives: 39.6 us -> none  [on_device(): peaks.append(lax.pmax(jnp.max(diagonal), ('grid', 'orb')))]
    dot_general x10 -> x0, matrix products: 27.5 us -> none  [the longest x4 20.1 us: contract_first(): lax.dot_general(left, right, (((0,), (0,)), ((), ())), preferred_element_...]
    unnamed x1 -> x0, blocking collectives: 12.2 us -> none
    unnamed x14 -> x6, local copies, waits for them, and re-layouts: 15.5 us -> 3.96 us
    all_gather x1 -> x0, blocking collectives: 10.8 us -> none  [on_device(): whole = lax.all_gather(local_pivots, 'orb', axis=0, tiled=True)]
  transfers between devices with their start and end apart: 4 -> 0, of which waited for: 2 -> 0; matrix products, arithmetic and copies ran while one was open for 31% -> 0% of each run, Pallas kernels for 0% -> 0%
where the time goes in v1:
time: 105 us
  Pallas kernels  98.1 us (93%)
  local copies, waits for them, and re-layouts  6.1 us (6%)
    pallas_call x1, Pallas kernels, on_device(): pl.pallas_call(functools.partial(kernel, n_grid, n_orb, steps, depth * n_...  98.1 us
    unnamed x6, local copies, waits for them, and re-layouts  3.96 us

profile of v1, /device:TPU:0, one launch (start us, length us, event | category | flops | bytes accessed | tf_op | source)
XLA Modules:
  0.0 104.8 jit_solution(9728465617401898855)
XLA Ops:
  0.6 1.5 %reshape.14.piv_ref = s32[288,1]{1,0:T(8,128)} reshape(s32[3,96]{1,0:T(4,128)} %param.3) | data formatting | bytes 2304 | tf_op jit(solution)/shard_map/reshape | solution.py:390
  2.1 98.1 %shard_map.49 = (f32[2048,288]{1,0:T(8,128)}, f32[1,2048]{1,0:T(1,128)}, f32[8,128]{1,0:T(8,128)}) custom-call(bf16[450,8192]{1,0:T(8,128)(2,1)} %orb_hbm.1, s32[288,1]{1,0:T(8,128)} %reshape.14.piv_ref), custom_call_target="tpu_custom_call" | custom-call | tf_op jit(solution)/shard_map/pallas_call | solution.py:349
  100.2 0.0 copy-start.1
  100.2 0.0 copy-start
  100.2 3.4 %copy.7 = f32[2048,288]{0,1:T(8,128)} copy(f32[2048,288]{1,0:T(8,128)} %get-tuple-element.12) | data formatting | bytes 4718592
  103.6 0.0 copy-done.1
  103.6 0.6 slice_reduce_fusion
  104.2 0.0 copy-done
  104.2 0.6 copy.9
Async XLA Ops:
  100.2 3.4 %copy-start.1 = (f32[8,128]{1,0:T(8,128)S(1)}, f32[8,128]{1,0:T(8,128)}, u32[]{:S(2)}) copy-start(f32[8,128]{1,0:T(8,128)} %get-tuple-element.8) | copy-start | bytes 12292
  100.2 4.0 %copy-start = (f32[1,2048]{1,0:T(1,128)S(1)}, f32[1,2048]{1,0:T(1,128)}, u32[]{:S(2)}) copy-start(f32[1,2048]{1,0:T(1,128)} %get-tuple-element.7) | copy-start | bytes 24580

commit v2 on v1

--- a/solution.py
+++ b/solution.py
@@ -47,10 +47,10 @@
     n_grid, n_orb, steps, orbitals_count,
     orb_hbm, piv_ref,
     factor_hbm, diag_ref, peaks_ref,
-    own, other, mine, total, heard, swap, sums, arrived, local, pair_send, pair_recv,
+    own, other, mine, total, heard, swap, sums, arrived, side_sums, side_arrived, local, pair_send, pair_recv,
     aug, out_v, tile_mine, tile_orb, tile_grid,
     load_sem, out_sem, x_send, x_recv, p1_send, p1_recv, p2_send, p2_recv,
-    c_send, c_recv, q_send, q_recv, h_send, h_recv, s_send, s_recv,
+    c_send, c_recv, q_send, q_recv, h_send, h_recv, s_send, s_recv, z_send, z_recv,
     mo_send, mo_recv, mg_send, mg_recv,
 ):
     g = lax.axis_index("grid")
@@ -151,6 +151,29 @@
             second(d).start()
         total[lax.rem(g, slots)] = added
 
+    for copy in crossing:
+        copy.wait_recv()
+
+    def moments(block, yy, p):
+        lo = p * part
+        a = own[block, :, lo : lo + part]
+        b = other[yy, :, lo : lo + part]
+        a32 = a.astype(F32)
+        b32 = b.astype(F32)
+        squares = jnp.sum(a32 * a32, axis=0, keepdims=True) + jnp.sum(
+            b32 * b32, axis=0, keepdims=True
+        )
+        point_sum = jnp.sum(a32, axis=0, keepdims=True) + jnp.sum(b32, axis=0, keepdims=True)
+        return squares, point_sum
+
+    for p in range(PARTS):
+        squares, point_sum = moments(across, 1 - side, p)
+        side_sums[p] = jnp.zeros((8, part), F32)
+        side_sums[p, 0:1] = squares
+        side_sums[p, 1:2] = point_sum
+        squares, _ = moments(o, side, p)
+        local[p, rank : rank + 8, :] = jnp.broadcast_to(squares, (8, part))
+
     for d in range(1, n_grid):
         source = lax.rem(g + n_grid - d, n_grid)
 
@@ -169,41 +192,51 @@
     there = jnp.reshape(swap[...], (rank, swap.shape[2]))
     pair = pair_here + dot_nt(there, there)
     half = rank // 2
+    pivot_mean = (
+        jnp.sum(here.astype(F32), axis=1, keepdims=True)
+        + jnp.sum(there.astype(F32), axis=1, keepdims=True)
+    ) / (2.0 * total.shape[2])
     for h in range(2):
-        pair_send[h] = pair[h * half : (h + 1) * half]
+        pair_send[h, :, 0:rank] = pair[h * half : (h + 1) * half]
+        pair_send[h, :, rank : rank + 1] = pivot_mean[h * half : (h + 1) * half]
     pair_copy = pltpu.make_async_remote_copy(
         src_ref=pair_send.at[core], dst_ref=pair_recv.at[0], send_sem=q_send, recv_sem=q_recv,
         device_id=(g, across), device_id_type=MESH,
     )
     pair_copy.start()
-
-    for copy in crossing:
-        copy.wait_recv()
 
     def products(block, yy, p):
         lo = p * part
         a = own[block, :, lo : lo + part]
         b = other[yy, :, lo : lo + part]
-        inner = dot_nn(here, a) + dot_nn(there, b)
-        a32 = a.astype(F32)
-        b32 = b.astype(F32)
-        squares = jnp.sum(a32 * a32, axis=0, keepdims=True) + jnp.sum(
-            b32 * b32, axis=0, keepdims=True
-        )
-        return inner, squares
+        return dot_nn(here, a) + dot_nn(there, b)
+
 
     travel = []
     for p in range(PARTS):
-        inner, squares = products(across, 1 - side, p)
-        sums[p, 0:rank, :] = inner
-        sums[p, rank : rank + 8, :] = jnp.broadcast_to(squares, (8, part))
-        copy = pltpu.make_async_remote_copy(
-            src_ref=sums.at[p], dst_ref=arrived.at[p],
-            send_sem=s_send.at[p], recv_sem=s_recv.at[p],
-            device_id=(g, across), device_id_type=MESH,
-        )
-        copy.start()
-        travel.append(copy)
+        inner = products(across, 1 - side, p)
+        squares = side_sums[p, 0:1]
+        point_sum = side_sums[p, 1:2]
+        rest = inner - pivot_mean * point_sum
+        most = jnp.max(jnp.abs(rest), axis=0, keepdims=True)
+        step = jnp.maximum(most * (1.0 / 32767.0), 1e-30)
+        coded = jnp.round(rest * (1.0 / step))
+        sums[p] = jnp.clip(coded, -32767.0, 32767.0).astype(jnp.int32).astype(jnp.int16)
+        side_sums[p, 2:3] = step
+        for copy in (
+            pltpu.make_async_remote_copy(
+                src_ref=side_sums.at[p], dst_ref=side_arrived.at[p],
+                send_sem=z_send.at[p], recv_sem=z_recv.at[p],
+                device_id=(g, across), device_id_type=MESH,
+            ),
+            pltpu.make_async_remote_copy(
+                src_ref=sums.at[p], dst_ref=arrived.at[p],
+                send_sem=s_send.at[p], recv_sem=s_recv.at[p],
+                device_id=(g, across), device_id_type=MESH,
+            ),
+        ):
+            copy.start()
+            travel.append(copy)
 
     pair_copy.wait_recv()
     half_copy = pltpu.make_async_remote_copy(
@@ -212,22 +245,17 @@
     )
     half_copy.start()
     for p in range(PARTS):
-        inner, squares = products(o, side, p)
-        local[p, 0:rank, :] = inner
-        local[p, rank : rank + 8, :] = jnp.broadcast_to(squares, (8, part))
+        local[p, 0:rank, :] = products(o, side, p)
     half_copy.wait_recv()
     first_half = jnp.where(core == 0, pair_recv[0], pair_recv[1])
     second_half = jnp.where(core == 0, pair_recv[1], pair_recv[0])
-    wide = aug.shape[1] // 2
-    aug[:, wide:] = jnp.where(
-        lax.broadcasted_iota(jnp.int32, (rank, wide), 0)
-        == lax.broadcasted_iota(jnp.int32, (rank, wide), 1),
-        1.0,
-        0.0,
-    )
-    aug[:, :wide] = jnp.zeros((rank, wide), F32)
-    aug[0:half, 0:rank] = jnp.square((pair_send[0] + first_half) / orbitals_count)
-    aug[half:rank, 0:rank] = jnp.square((pair_send[1] + second_half) / orbitals_count)
+    wide = aug.shape[1]
+    aug[...] = jnp.zeros((rank, wide), F32)
+    aug[0:half, 0:rank] = jnp.square((pair_send[0] + first_half)[:, 0:rank] / orbitals_count)
+    aug[half:rank, 0:rank] = jnp.square((pair_send[1] + second_half)[:, 0:rank] / orbitals_count)
+    far_mean = jnp.concatenate(
+        [first_half[:, rank : rank + 1], second_half[:, rank : rank + 1]], axis=0
+    )
 
     def block_step(j, carry):
         start = pl.multiple_of(j * BLOCK, BLOCK)
@@ -240,30 +268,42 @@
         )
         lane = lax.broadcasted_iota(jnp.int32, (BLOCK, 128), 1)
         row_at = lax.broadcasted_iota(jnp.int32, (BLOCK, 128), 0)
-        square = dot_nn(strip[:, :wide], pick, HIGHEST)
+        square = dot_nn(strip, pick, HIGHEST)
         tile = jnp.where(lane < BLOCK, square, jnp.where(lane == row_at + 64, 1.0, 0.0))
         tile = eliminate_small(tile, BLOCK)
         inverse = tile[:, 64 : 64 + BLOCK]
-        solved = dot_nn(inverse, strip, HIGHEST)
-        head = solved[:, :wide]
-        ahead = lax.broadcasted_iota(jnp.int32, (BLOCK, wide), 1) >= start + BLOCK
-        multipliers = jnp.where(ahead, head, 0.0)
-        aug[...] = aug[...] - dot_tn(multipliers, solved, HIGHEST)[0:rank]
-        aug[pl.ds(start, BLOCK), :] = solved
+        at = lax.broadcasted_iota(jnp.int32, (BLOCK, wide), 1)
+        unit = jnp.where(at == lax.broadcasted_iota(jnp.int32, (BLOCK, wide), 0) + start, 1.0, 0.0)
+        solved = dot_nn(
+            inverse, jnp.where((at >= start) & (at < start + BLOCK), unit, strip), HIGHEST
+        )
+        multipliers = jnp.where(at >= start + BLOCK, solved, 0.0)
+        every_lane = lax.broadcasted_iota(jnp.int32, (rank, wide), 1)
+        every_row = lax.broadcasted_iota(jnp.int32, (rank, wide), 0)
+        clear = (
+            (every_lane >= start) & (every_lane < start + BLOCK) & (every_row >= start + BLOCK)
+        )
+        aug[...] = jnp.where(clear, 0.0, aug[...]) - dot_tn(multipliers, solved, HIGHEST)[0:rank]
+        aug[pl.ds(start, BLOCK), :] = jnp.where(at < start + BLOCK, solved, 0.0)
         return carry
 
     lax.fori_loop(0, rank // BLOCK, block_step, 0)
-    lower_inverse = aug[:, wide:]
+    lower_inverse = aug[...]
 
     count = rank // steps
     best = [None] * steps
     stores = []
     for p in range(PARTS):
-        travel[p].wait_recv()
-        both = local[p] + arrived[p]
-        scaled = jnp.square(both / orbitals_count)
-        columns = scaled[0:rank]
-        diagonal = scaled[rank : rank + 1]
+        travel[2 * p].wait_recv()
+        travel[2 * p + 1].wait_recv()
+        far = side_arrived[p]
+        inner = (
+            local[p, 0:rank, :]
+            + arrived[p].astype(jnp.int32).astype(F32) * far[2:3]
+            + far_mean * far[1:2]
+        )
+        columns = jnp.square(inner / orbitals_count)
+        diagonal = jnp.square((local[p, rank : rank + 1, :] + far[0:1]) / orbitals_count)
         solved = dot_nn(lower_inverse[:, 0:rank], columns, HIGHEST)
         out_v[p] = solved.T
         store = pltpu.make_async_copy(
@@ -369,12 +409,14 @@
                 vmem((slots, slot_rows, depth), BF16),
                 vmem((n_grid, slot_rows, depth), BF16),
                 vmem((slots, slot_rows, depth), BF16),
+                vmem((PARTS, rank, part), jnp.int16),
+                vmem((PARTS, rank, part), jnp.int16),
+                vmem((PARTS, 8, part), F32),
+                vmem((PARTS, 8, part), F32),
                 vmem((PARTS, rank + 8, part), F32),
-                vmem((PARTS, rank + 8, part), F32),
-                vmem((PARTS, rank + 8, part), F32),
-                vmem((2, rank // 2, rank), F32),
-                vmem((2, rank // 2, rank), F32),
-                vmem((rank, 2 * wide), F32),
+                vmem((2, rank // 2, rank + 1), F32),
+                vmem((2, rank // 2, rank + 1), F32),
+                vmem((rank, wide), F32),
                 vmem((PARTS, part, rank), F32),
                 vmem((2, 8, 128), F32),
                 vmem((n_orb, 8, 128), F32),
@@ -382,6 +424,7 @@
                 dma((n_orb,)), dma((PARTS,)), dma((2,)), dma((2,)),
                 dma((n_grid,)), dma((n_grid,)), dma((n_grid,)), dma((n_grid,)),
                 dma, dma, dma, dma, dma, dma, dma((PARTS,)), dma((PARTS,)),
+                dma((PARTS,)), dma((PARTS,)),
                 dma((n_orb,)), dma((n_orb,)), dma((n_grid,)), dma((n_grid,)),
             ],
             compiler_params=pltpu.CompilerParams(

time: 105 us -> 90.9 us (0.87)
  Pallas kernels: 98.1 us -> 83.9 us
    pallas_call x1, Pallas kernels: 98.1 us -> 83.9 us  [on_device(): pl.pallas_call(functools.partial(kernel, n_grid, n_orb, steps, depth * n_...]
where the time goes in v2:
time: 90.9 us; the launch traced here: 90.7 us
  Pallas kernels  83.9 us (92%)
  local copies, waits for them, and re-layouts  6.1 us (7%)
    pallas_call x1, Pallas kernels, on_device(): pl.pallas_call(functools.partial(kernel, n_grid, n_orb, steps, depth * n_...  83.9 us
    unnamed x6, local copies, waits for them, and re-layouts  3.96 us

profile of v2, /device:TPU:0, one launch (start us, length us, event | category | flops | bytes accessed | tf_op | source)
XLA Modules:
  0.0 90.7 jit_solution(5025541913469432865)
XLA Ops:
  0.6 1.5 %reshape.14.piv_ref = s32[288,1]{1,0:T(8,128)} reshape(s32[3,96]{1,0:T(4,128)} %param.3) | data formatting | bytes 2304 | tf_op jit(solution)/shard_map/reshape | solution.py:433
  2.1 83.9 %shard_map.49 = (f32[2048,288]{1,0:T(8,128)}, f32[1,2048]{1,0:T(1,128)}, f32[8,128]{1,0:T(8,128)}) custom-call(bf16[450,8192]{1,0:T(8,128)(2,1)} %orb_hbm.1, s32[288,1]{1,0:T(8,128)} %reshape.14.piv_ref), custom_call_target="tpu_custom_call" | custom-call | tf_op jit(solution)/shard_map/pallas_call | solution.py:389
  86.1 0.0 copy-start.1
  86.1 0.0 copy-start
  86.1 3.4 %copy.7 = f32[2048,288]{0,1:T(8,128)} copy(f32[2048,288]{1,0:T(8,128)} %get-tuple-element.12) | data formatting | bytes 4718592
  89.5 0.0 copy-done.1
  89.5 0.6 slice_reduce_fusion
  90.1 0.0 copy-done
  90.1 0.6 copy.9
Async XLA Ops:
  86.1 3.4 %copy-start.1 = (f32[8,128]{1,0:T(8,128)S(1)}, f32[8,128]{1,0:T(8,128)}, u32[]{:S(2)}) copy-start(f32[8,128]{1,0:T(8,128)} %get-tuple-element.8) | copy-start | bytes 12292
  86.1 4.0 %copy-start = (f32[1,2048]{1,0:T(1,128)S(1)}, f32[1,2048]{1,0:T(1,128)}, u32[]{:S(2)}) copy-start(f32[1,2048]{1,0:T(1,128)} %get-tuple-element.7) | copy-start | bytes 24580
